TPU v7x, 32 devices: a whole 2x2x4 slice. The times are simulated.
32 devices in a mesh: fsdp: 16 (over z, y, x), tp: 2 (over core).
Axes of the slice: x: 2, y: 2, z: 4, core: 2. Of those that a mesh axis runs over, the one named last changes fastest.
Arguments:
- inputs: bfloat16 [4096, 4096], P('fsdp'), may hold values from -6 to 6
- value_grad: bfloat16 [4096, 1024], P('fsdp', 'tp'), may hold values from -24 to 24
- value_weight: bfloat16 [4096, 1024], P('tp', 'fsdp'), may hold values from -0.09375 to 0.09375
- counts: int32 [16, 4], P('fsdp'), may hold values from 1 to 232, as said below
- offsets: int32 [16, 4], P('fsdp'), may hold values from 0 to 248, as said below
Outputs:
- input_grad: bfloat16 [4096, 4096], P('fsdp', 'tp')
- weight_grad: float32 [4096, 1024], P('fsdp', 'tp')
Inputs may be any that keep to these rules, and one draw needn't show every extreme that they name: `offsets`: on each index of fsdp the 4 samples lie in order; each starts at a multiple of 8, at or after the 8-row-aligned end of the previous one, and all lie within the 256 rows; on some index the aligned blocks of its samples fill all 256 rows. `counts`: how many rows the samples of a row group fill varies widely between indices of fsdp.
All inputs are finite; a program needn't handle non-finite values.
Results may differ from a plain program's by a relative error of at most 0.0046.
Values may be sent and summed in bfloat16 or wider, within the bound.
A program may use at most 64 MiB of HBM per device.

v0:
```python
import math
import jax
import jax.numpy as jnp
from jax import lax
from jax.sharding import PartitionSpec as P


def local(inputs, value_grad, value_weight, counts, offsets):
    tok_rows = inputs.shape[0]
    row_block = min(128, tok_rows)
    positions = jnp.arange(tok_rows, dtype=jnp.int32)[:, None]
    starts = offsets[0][None, :]
    lengths = counts[0][None, :]
    inside = (positions >= starts) & (positions < starts + lengths)
    inverse_root = lax.rsqrt(lengths.astype(jnp.float32))
    row_factor = jnp.sum(jnp.where(inside, inverse_root, jnp.zeros_like(inverse_root)), axis=1)
    scaled = (value_grad.astype(jnp.float32) * row_factor[:, None]).astype(jnp.bfloat16)
    live_end = jnp.max(offsets[0] + counts[0])
    live_blocks = (live_end + row_block - 1) // row_block
    scaled_all = lax.all_gather(scaled, "tp", axis=1, tiled=True)
    empty_inputs = jnp.zeros((tok_rows, value_weight.shape[0]), jnp.float32)
    piece = lax.all_gather(value_weight, "fsdp", axis=1, tiled=True)

    def add_add_block(block_index, partial_value):
        lower = lax.dynamic_slice_in_dim(scaled_all, block_index * row_block, row_block, 0)
        before = lax.dynamic_slice_in_dim(partial_value, block_index * row_block, row_block, 0)
        product = lax.dot_general(
            lower, piece, (((1,), (1,)), ((), ())), preferred_element_type=jnp.float32
        )
        return lax.dynamic_update_slice_in_dim(
            partial_value, before + product, block_index * row_block, 0
        )

    result = lax.fori_loop(0, live_blocks, add_add_block, empty_inputs)
    input_grad = result.astype(jnp.bfloat16)
    normalizer = 1.0 / math.sqrt(counts.shape[1] * lax.axis_size("fsdp"))
    empty = jnp.zeros((inputs.shape[1], scaled.shape[1]), jnp.float32)

    def weight_add_block(block_index, partial_value):
        feature_rows = lax.dynamic_slice_in_dim(inputs, block_index * row_block, row_block, 0)
        grad_rows = lax.dynamic_slice_in_dim(scaled, block_index * row_block, row_block, 0)
        return partial_value + lax.dot_general(
            feature_rows, grad_rows, (((0,), (0,)), ((), ())), preferred_element_type=jnp.float32
        )

    result = lax.fori_loop(0, live_blocks, weight_add_block, empty)
    summed = lax.psum_scatter(result, "fsdp", scatter_dimension=0, tiled=True)
    return (input_grad, summed * normalizer)


def solution(mesh):
    in_specs = (P("fsdp", None), P("fsdp", "tp"), P("tp", "fsdp"), P("fsdp", None), P("fsdp", None))
    out_specs = (P("fsdp", "tp"), P("fsdp", "tp"))
    return jax.shard_map(local, mesh=mesh, in_specs=in_specs, out_specs=out_specs, check_vma=False)
```

profile of v0, /device:TPU:10, one launch (start us, length us, event | category | flops | bytes accessed | tf_op | source)
XLA Modules:
  0.0 278.1 jit_solution(10683928178615963049)
XLA Ops:
  7.2 0.0 all-gather.2.cloned.1.call-start
  7.2 0.7 all-gather.2.cloned.1.call-update
  7.9 0.0 reduce-scatter.2.cloned.1.call-start
  7.9 1.3 fusion.7
  9.9 0.7 rsqrt_bitcast_fusion
  10.6 0.7 add_bitcast_fusion
  11.3 0.7 select_reduce_fusion
  12.0 1.1 multiply_convert_fusion
  13.1 0.0 copy-start
  13.1 4.3 %broadcast_in_dim.30 = f32[4096,512]{1,0:T(8,128)} broadcast(f32[]{:T(128)} %constant.38.clone.1), dimensions={} | broadcast | bytes 8388612 | tf_op jit(solution)/shard_map/broadcast_in_dim | solution.py:37
  17.4 0.0 copy-done
  17.4 8.0 %while.21 = (s32[]{:T(128)}, f32[4096,512]{1,0:T(8,128)}, s32[]{:T(128)}, bf16[256,4096]{1,0:T(8,128)(2,1)S(1)}, bf16[256,512]{1,0:T(8,128)(2,1)S(1)}, /*index=5*/s32[]{:T(128)}, s32[]{:T(128)}, s32[]{:T(128)}, s32[]{:T(128)}) while((s32[]{:T(128)}, f32[4096,512]{1,0:T(8,128)}, s32[]{:T(128)}, bf16[256,4096]{1,0:T(8,128)(2,1)S(1)}, ...), condition=%wide.region_5.6_spmd, body=%wide.region_4.5_spmd.sunk | while | flops 538968064 | bytes 17958028 | solution.py:46
  17.4 8.0 %convolution_add_fusion.3 = f32[4096,512]{1,0:T(8,128)} fusion(f32[4096,512]{1,0:T(8,128)} %get-tuple-element.191, bf16[256,4096]{1,0:T(8,128)(2,1)S(1)} %get-tuple-element.202, s32[]{:T(128)S(6)} %select_n.24, bf16[256,512]{1,0:T(8,128)(2,1)S(1)} %get-tuple-element.203), kind=kOutput, calls=%fused_computation.4.clone.1 | convolution fusion | flops 538968064 | bytes 17957888 | tf_op jit(solution)/shard_map/while/body/dot_general | solution.py:42
  25.4 0.0 reduce-scatter.2.cloned.1.call-update
  25.4 2.2 all_gather.6
  27.6 59.9 %all-gather.2.cloned.1.call-done = bf16[2048,1024]{0,1:T(8,128)(2,1)} async-done(((bf16[2048,64]{0,1:T(8,128)(2,1)}), bf16[2048,1024]{0,1:T(8,128)(2,1)}) %all-gather.2.cloned.1.call-update) | async-done | bytes 4194320 | tf_op jit(solution)/shard_map/all_gather | solution.py:22
  87.5 6.4 %copy.9 = bf16[2048,1024]{1,0:T(8,128)(2,1)} copy(bf16[2048,1024]{0,1:T(8,128)(2,1)} %all-gather.2.cloned.1.call-done) | data formatting | bytes 8388608 | tf_op jit(solution)/shard_map/while | solution.py:34
  93.9 0.2 broadcast_in_dim.26
  94.1 4.0 %while.20 = (s32[]{:T(128)}, f32[256,2048]{1,0:T(8,128)S(1)}, s32[]{:T(128)}, bf16[256,1024]{1,0:T(8,128)(2,1)S(1)}, bf16[2048,1024]{1,0:T(8,128)(2,1)}, /*index=5*/s32[]{:T(128)}, s32[]{:T(128)}, s32[]{:T(128)}, s32[]{:T(128)}) while((s32[]{:T(128)}, f32[256,2048]{1,0:T(8,128)S(1)}, s32[]{:T(128)}, bf16[256,1024]{1,0:T(8,128)(2,1)S(1)}, ...), condition=%wide.region_3.4_spmd, body=%wide.region_2.3_spmd.sunk | while | flops 537133056 | bytes 6554763 | solution.py:34
  94.2 4.0 %fusion.16 = f32[256,2048]{1,0:T(8,128)S(1)} fusion(f32[256,2048]{1,0:T(8,128)S(1)} %get-tuple-element.164, s32[]{:T(128)S(6)} %select_n.23, bf16[2048,1024]{1,0:T(8,128)(2,1)} %get-tuple-element.176, bf16[256,1024]{1,0:T(8,128)(2,1)S(1)} %get-tuple-element.175), kind=kOutput, calls=%fused_computation.1.clone.1 | convolution fusion | flops 537133056 | bytes 6554624 | tf_op jit(solution)/shard_map/while/body/dot_general | solution.py:27
  98.1 1.1 convert_element_type.15
  99.3 170.2 %reduce-scatter.2.cloned.1.call-done = f32[256,512]{1,0:T(8,128)} async-done(((f32[4096,512]{1,0:T(8,128)}), f32[256,512]{1,0:T(8,128)}) %reduce-scatter.2.cloned.1.call-update) | async-done | bytes 524304 | tf_op jit(solution)/shard_map/reduce_scatter | solution.py:47
  269.4 1.9 broadcast_multiply_fusion
Async XLA Ops:
  7.2 80.3 %all-gather.2.cloned.1.call-start = ((), (), s32[]{:S(2)}) async-start(), calls=%async_computation.1 | async-start | bytes 4456448 | tf_op jit(solution)/shard_map/all_gather | solution.py:22
  7.9 261.5 %reduce-scatter.2.cloned.1.call-start = ((), (), s32[]{:S(2)}) async-start(), calls=%async_computation.2 | async-start | bytes 8912896 | tf_op jit(solution)/shard_map/reduce_scatter | solution.py:47
  13.1 4.3 %copy-start = (bf16[256,4096]{1,0:T(8,128)(2,1)S(1)}, bf16[256,4096]{1,0:T(8,128)(2,1)}, u32[]{:S(2)}) copy-start(bf16[256,4096]{1,0:T(8,128)(2,1)} %param.9) | copy-start | bytes 6291460
Sparse Core Ops, SparseCore 0:
  10.7 76.6 all-gather.1
  89.8 179.6 reduce-scatter.1
where the time goes:
time: 279 us; the launch traced here: 278 us
  waiting for transfers between devices  231 us (83%)
  between operations  14.7 us (5%)
  matrix products  12 us (4%)
  local copies, waits for them, and re-layouts  10.9 us (4%)
  other arithmetic  7.43 us (3%)
    reduce_scatter x1, waiting for transfers between devices, local(): summed = lax.psum_scatter(result, 'fsdp', scatter_dimension=0, tiled=True)  170 us
    all_gather x1, waiting for transfers between devices, local(): piece = lax.all_gather(value_weight, 'fsdp', axis=1, tiled=True)  59.9 us
    dot_general x1, matrix products, weight_add_block(): lax.dot_general(feature_rows, grad_rows, (((0,), (0,)), ((), ())), prefer...  7.98 us
    while x1, local copies, waits for them, and re-layouts, local(): result = lax.fori_loop(0, live_blocks, add_add_block, empty_inputs)  6.42 us
  transfers between devices with their start and end apart: 2, of which 2 were waited for; matrix products, arithmetic and copies ran while one was open for 10% of the time, Pallas kernels for 0%

commit v1 on v0

--- a/solution.py
+++ b/solution.py
@@ -19,7 +19,8 @@
     live_blocks = (live_end + row_block - 1) // row_block
     scaled_all = lax.all_gather(scaled, "tp", axis=1, tiled=True)
     empty_inputs = jnp.zeros((tok_rows, value_weight.shape[0]), jnp.float32)
-    piece = lax.all_gather(value_weight, "fsdp", axis=1, tiled=True)
+    shards = lax.all_gather(value_weight, "fsdp")
+    piece = jnp.concatenate(shards, axis=1)
 
     def add_add_block(block_index, partial_value):
         lower = lax.dynamic_slice_in_dim(scaled_all, block_index * row_block, row_block, 0)

time: 279 us -> 279 us (level)
  local copies, waits for them, and re-layouts: 10.9 us -> 19.8 us
  waiting for transfers between devices: 231 us -> 223 us
    reduce_scatter x1, waiting for transfers between devices: 170 us -> 162 us  [local(): summed = lax.psum_scatter(result, 'fsdp', scatter_dimension=0, tiled=True)]
    unnamed x2 -> x3, local copies, waits for them, and re-layouts: 0.01 us -> 4.59 us
    reshape x0 -> x1, local copies, waits for them, and re-layouts: none -> 4.25 us  [local(): piece = jnp.concatenate(shards, axis=1)]
  transfers between devices with their start and end apart: 2 -> 2, of which waited for: 2 -> 2; matrix products, arithmetic and copies ran while one was open for 10% -> 13% of each run, Pallas kernels for 0% -> 0%
where the time goes in v1:
time: 279 us
  waiting for transfers between devices  223 us (80%)
  local copies, waits for them, and re-layouts  19.8 us (7%)
  between operations  14.7 us (5%)
  matrix products  11.7 us (4%)
  other arithmetic  7.43 us (3%)
    reduce_scatter x1, waiting for transfers between devices, local(): summed = lax.psum_scatter(result, 'fsdp', scatter_dimension=0, tiled=True)  162 us
    all_gather x1, waiting for transfers between devices, local(): shards = lax.all_gather(value_weight, 'fsdp')  59.6 us
    dot_general x1, matrix products, weight_add_block(): lax.dot_general(feature_rows, grad_rows, (((0,), (0,)), ((), ())), prefer...  7.99 us
    while x1, local copies, waits for them, and re-layouts, local(): result = lax.fori_loop(0, live_blocks, add_add_block, empty_inputs)  6.42 us
  transfers between devices with their start and end apart: 2, of which 2 were waited for; matrix products, arithmetic and copies ran while one was open for 13% of the time, Pallas kernels for 0%

profile of v1, /device:TPU:10, one launch (start us, length us, event | category | flops | bytes accessed | tf_op | source)
XLA Modules:
  0.0 278.6 jit_solution(16639860792189114490)
XLA Ops:
  7.2 0.0 all-gather.3.cloned.1.call-start
  7.2 0.7 all-gather.3.cloned.1.call-update
  7.9 0.0 reduce-scatter.2.cloned.1.call-start
  7.9 1.3 fusion.7
  9.9 0.7 rsqrt_bitcast_fusion
  10.6 0.7 add_bitcast_fusion
  11.3 0.7 select_reduce_fusion
  12.0 1.1 multiply_convert_fusion
  13.1 0.0 copy-start
  13.1 4.3 %broadcast_in_dim.30 = f32[4096,512]{1,0:T(8,128)} broadcast(f32[]{:T(128)} %constant.38.clone.1), dimensions={} | broadcast | bytes 8388612 | tf_op jit(solution)/shard_map/broadcast_in_dim | solution.py:38
  17.4 0.0 copy-done
  17.4 8.0 %while.21 = (s32[]{:T(128)}, f32[4096,512]{1,0:T(8,128)}, s32[]{:T(128)}, bf16[256,4096]{1,0:T(8,128)(2,1)S(1)}, bf16[256,512]{1,0:T(8,128)(2,1)S(1)}, /*index=5*/s32[]{:T(128)}, s32[]{:T(128)}, s32[]{:T(128)}, s32[]{:T(128)}) while((s32[]{:T(128)}, f32[4096,512]{1,0:T(8,128)}, s32[]{:T(128)}, bf16[256,4096]{1,0:T(8,128)(2,1)S(1)}, ...), condition=%wide.region_5.6_spmd, body=%wide.region_4.5_spmd.sunk | while | flops 538968064 | bytes 17958028 | solution.py:47
  17.4 8.0 %convolution_add_fusion.3 = f32[4096,512]{1,0:T(8,128)} fusion(f32[4096,512]{1,0:T(8,128)} %get-tuple-element.196, bf16[256,4096]{1,0:T(8,128)(2,1)S(1)} %get-tuple-element.207, s32[]{:T(128)S(6)} %select_n.24, bf16[256,512]{1,0:T(8,128)(2,1)S(1)} %get-tuple-element.208), kind=kOutput, calls=%fused_computation.4.clone.1 | convolution fusion | flops 538968064 | bytes 17957888 | tf_op jit(solution)/shard_map/while/body/dot_general | solution.py:43
  25.4 0.0 reduce-scatter.2.cloned.1.call-update
  25.4 2.2 all_gather.9
  27.6 59.6 %all-gather.3.cloned.1.call-done = bf16[32768,64]{0,1:T(8,128)(2,1)} async-done(((bf16[2048,64]{0,1:T(8,128)(2,1)}), bf16[32768,64]{0,1:T(8,128)(2,1)}) %all-gather.3.cloned.1.call-update) | async-done | bytes 4194320 | tf_op jit(solution)/shard_map/all_gather | solution.py:22
  87.2 4.6 %copy.13 = bf16[8,8,16,2048]{3,2,1,0:T(8,128)(2,1)S(1)} copy(bf16[8,8,16,2048]{3,1,2,0:T(8,128)(2,1)} %bitcast.22) | data formatting | bytes 8388608
  91.8 4.3 %copy.11 = bf16[2048,16,64]{0,2,1:T(8,128)(2,1)} copy(bf16[2048,16,64]{0,1,2:T(8,128)(2,1)S(1)} %bitcast.20) | data formatting | bytes 8388608 | tf_op jit(solution)/shard_map/reshape | solution.py:23
  96.0 6.4 %copy.12 = bf16[2048,1024]{1,0:T(8,128)(2,1)} copy(bf16[2048,1024]{0,1:T(8,128)(2,1)} %bitcast.21) | data formatting | bytes 8388608 | tf_op jit(solution)/shard_map/while | solution.py:35
  102.5 0.2 broadcast_in_dim.26
  102.7 3.7 %while.20 = (s32[]{:T(128)}, f32[256,2048]{1,0:T(8,128)S(1)}, s32[]{:T(128)}, bf16[256,1024]{1,0:T(8,128)(2,1)S(1)}, bf16[2048,1024]{1,0:T(8,128)(2,1)}, /*index=5*/s32[]{:T(128)}, s32[]{:T(128)}, s32[]{:T(128)}, s32[]{:T(128)}) while((s32[]{:T(128)}, f32[256,2048]{1,0:T(8,128)S(1)}, s32[]{:T(128)}, bf16[256,1024]{1,0:T(8,128)(2,1)S(1)}, ...), condition=%wide.region_3.4_spmd, body=%wide.region_2.3_spmd.sunk | while | flops 537133056 | bytes 6554763 | solution.py:35
  102.7 3.7 %fusion.16 = f32[256,2048]{1,0:T(8,128)S(1)} fusion(f32[256,2048]{1,0:T(8,128)S(1)} %get-tuple-element.169, s32[]{:T(128)S(6)} %select_n.23, bf16[2048,1024]{1,0:T(8,128)(2,1)} %get-tuple-element.181, bf16[256,1024]{1,0:T(8,128)(2,1)S(1)} %get-tuple-element.180), kind=kOutput, calls=%fused_computation.1.clone.1 | convolution fusion | flops 537133056 | bytes 6554624 | tf_op jit(solution)/shard_map/while/body/dot_general | solution.py:28
  106.4 1.1 convert_element_type.15
  107.5 162.4 %reduce-scatter.2.cloned.1.call-done = f32[256,512]{1,0:T(8,128)} async-done(((f32[4096,512]{1,0:T(8,128)}), f32[256,512]{1,0:T(8,128)}) %reduce-scatter.2.cloned.1.call-update) | async-done | bytes 524304 | tf_op jit(solution)/shard_map/reduce_scatter | solution.py:48
  269.9 1.9 broadcast_multiply_fusion
Async XLA Ops:
  7.2 80.0 %all-gather.3.cloned.1.call-start = ((), (), s32[]{:S(2)}) async-start(), calls=%async_computation.2 | async-start | bytes 4456448 | tf_op jit(solution)/shard_map/all_gather | solution.py:22
  7.9 262.0 %reduce-scatter.2.cloned.1.call-start = ((), (), s32[]{:S(2)}) async-start(), calls=%async_computation.1 | async-start | bytes 8912896 | tf_op jit(solution)/shard_map/reduce_scatter | solution.py:48
  13.1 4.3 %copy-start = (bf16[256,4096]{1,0:T(8,128)(2,1)S(1)}, bf16[256,4096]{1,0:T(8,128)(2,1)}, u32[]{:S(2)}) copy-start(bf16[256,4096]{1,0:T(8,128)(2,1)} %param.9) | copy-start | bytes 6291460
Sparse Core Ops, SparseCore 0:
  10.7 76.4 all-gather.2
  89.5 180.3 reduce-scatter.1
